TPU v7x, 32 devices: a whole 2x2x4 slice. The times are simulated.
32 devices in a mesh: dp: 8 (over z, y), group: 4 (over x, core).
Axes of the slice: x: 2, y: 2, z: 4, core: 2. Of those that a mesh axis runs over, the one named last changes fastest.
Arguments:
- keys: int32 [16384], P(('dp', 'group')), may hold values from 0 to 1073741823
- cut: int32 [1], replicated, may hold values from 256 to 1023
- owner: int32 [16384, 1], P(('dp', 'group')), may hold values from 0 to 7; in each aligned block of 512 rows (0 to 511, 512 to 1023, ...) at most 128 rows name the same one
- tokens: int32 [16384, 2048], P(('dp', 'group')), may hold values from 0 to 128255
Outputs:
- histogram: int32 [4096], replicated
- packed_rows: int32 [32768, 2048], P(('dp', 'group'))
- packed_weights: float32 [32768], P(('dp', 'group'))
Inputs may be any that keep to these rules, and one draw needn't show every extreme that they name: Among the examples of one device, at most 128 have the same owner, and some owner has exactly 128.
All inputs are finite; a program needn't handle non-finite values.
Results may differ from a plain program's by a relative error of at most 0.0003.
Values sent between devices are 32-bit elements; how exact they have to be, the bound alone decides.
A program may use at most 128 MiB of HBM per device.

v0:
```python
import jax
import jax.numpy as jnp
from jax import lax
from jax.sharding import PartitionSpec as P

BINS = 4096
BIN_WIDTH = 262144


def body(keys, cut, owner, tokens):
    examples = keys.shape[0]
    width = tokens.shape[1]
    n_owner = lax.axis_size("dp")
    n_member = lax.axis_size("group")
    slots = 2 * examples // (n_owner * n_member)
    capacity = 2 * examples
    bins_of = keys // BIN_WIDTH
    local_hist = jnp.zeros((BINS,), jnp.float32).at[bins_of].add(1.0)
    kept = bins_of >= cut[0]
    dest = owner[:, 0]
    onehot = (
        (dest[:, None] == jnp.arange(n_owner, dtype=jnp.int32)[None, :]) & kept[:, None]
    ).astype(jnp.int32)
    counts = jnp.sum(onehot, axis=0).astype(jnp.float32)
    table = lax.all_gather(counts[None, :], ("dp", "group"), axis=0, tiled=True)
    position = lax.axis_index(("dp", "group"))
    below = jnp.arange(table.shape[0], dtype=jnp.int32) < position
    before = jnp.sum(jnp.where(below[:, None], table, 0.0), axis=0)
    hist = lax.psum(local_hist, ("dp", "group"))
    running = jnp.cumsum(onehot, axis=0) - onehot
    local_rank = jnp.sum(running * onehot, axis=1)
    offset = jnp.sum(before.astype(jnp.int32)[None, :] * onehot, axis=1)
    rank = offset + local_rank
    member = rank % n_member
    outside = n_owner * n_member * slots
    position_send = jnp.where(
        kept, (dest * n_member + member) * slots + local_rank // n_member, outside
    )
    send_rows = jnp.zeros((outside, width), jnp.int32).at[position_send].set(tokens, mode="drop")
    details = jnp.stack([rank // n_member, keys], axis=1)
    send_meta = jnp.full((outside, 2), -1, jnp.int32).at[position_send].set(details, mode="drop")
    send_rows = send_rows.reshape(n_owner, n_member, slots, width)
    send_meta = send_meta.reshape(n_owner, n_member, slots, 2)
    got_rows, got_meta = (
        lax.all_to_all(
            lax.all_to_all(send_rows, "dp", split_axis=0, concat_axis=0, tiled=True),
            "group",
            split_axis=1,
            concat_axis=1,
            tiled=True,
        ),
        lax.all_to_all(
            lax.all_to_all(send_meta, "dp", split_axis=0, concat_axis=0, tiled=True),
            "group",
            split_axis=1,
            concat_axis=1,
            tiled=True,
        ),
    )
    got_rows = got_rows.reshape(-1, width)
    got_meta = got_meta.reshape(-1, 2)
    slot = got_meta[:, 0]
    valid = slot >= 0
    target = jnp.where(valid, slot, capacity)
    suffix = jnp.cumsum(hist[::-1])[::-1]
    total = jnp.maximum(suffix[cut[0]], 1.0)
    got_bins = jnp.clip(got_meta[:, 1] // BIN_WIDTH, 0, BINS - 1)
    weight = jnp.where(valid, suffix[got_bins] / total, 0.0)
    packed_rows = jnp.zeros((capacity, width), jnp.int32).at[target].set(got_rows, mode="drop")
    packed_weights = jnp.zeros((capacity,), jnp.float32).at[target].set(weight, mode="drop")
    return (hist.astype(jnp.int32), packed_rows, packed_weights)


def solution(mesh):
    placed = (P(("dp", "group")), P(), P(("dp", "group"), None), P(("dp", "group"), None))
    return jax.shard_map(
        body,
        mesh=mesh,
        in_specs=placed,
        out_specs=(P(), P(("dp", "group"), None), P(("dp", "group"))),
        check_vma=False,
    )
```

profile of v0, /device:TPU:0, one launch (start us, length us, event | category | flops | bytes accessed | tf_op | source)
XLA Modules:
  0.0 387.2 jit_solution(11714940786831163853)
XLA Ops:
  1.3 0.7 broadcast_compare_fusion
  2.0 0.8 convert_reduce_fusion
  2.8 3.3 scatter_custom_fusion
  6.2 42.1 %all-reduce.1 = (f32[4096]{0:T(1024)S(1)}, f32[256]{0:T(256)S(1)}) all-reduce(f32[4096]{0:T(1024)S(1)} %scatter_custom_fusion, f32[256]{0:T(256)S(1)} %convert_dynamic-update-slice_fusion), channel_id=1, replica_groups=mesh['dp'=8,'group'=4] {'dp','group'}, use_global_device_ids=true, to_apply=%region_1.2 | all-reduce | flops 4352 | bytes 34816 | tf_op jit(solution)/shard_map/psum | solution.py:29
  48.5 0.7 fusion.10
  49.2 1.1 reduce-window.15
  50.3 0.2 slice_reduce_fusion.1
  50.6 0.8 select_reduce_fusion
  51.4 0.7 compare_select_fusion.6
  52.1 0.7 pad_add_fusion
  52.9 1.8 scatter_custom_fusion.1
  54.8 0.3 copy.20
  55.0 0.7 reshape.203
  55.7 5.3 %all-to-all-start = ((s32[8,1,256]{2,1,0:T(1,128)}), s32[8,1,256]{2,1,0:T(1,128)S(1)}, u32[]{:S(2)}, u32[]{:S(2)}) async-start(s32[8,1,256]{2,1,0:T(1,128)} %reshape.203), calls=%async_computation | async-start | bytes 16384 | tf_op jit(solution)/shard_map/all_to_all | solution.py:53
  61.1 8.6 %scatter_custom_fusion.2 = s32[1024,2048]{1,0:T(8,128)} fusion(s32[512]{0:T(512)S(1)} %get-tuple-element.7, s32[512,2048]{1,0:T(8,128)} %param.7, s32[]{:T(128)} %constant.83.clone.1), kind=kCustom, calls=%fused_computation.8 | custom fusion | bytes 8389120 | tf_op jit(solution)/shard_map/scatter | solution.py:39
  69.7 6.0 %all-to-all-start.2 = ((s32[8,4,32,2048]{3,2,1,0:T(8,128)}), s32[8,4,32,2048]{3,2,1,0:T(8,128)}, u32[]{:S(2)}, u32[]{:S(2)}) async-start(s32[8,4,32,2048]{3,2,1,0:T(8,128)} %bitcast.35), calls=%async_computation.2 | async-start | bytes 16777216 | tf_op jit(solution)/shard_map/all_to_all | solution.py:46
  75.7 0.5 broadcast.157
  76.2 0.6 reduce.6
  76.9 0.7 reshape.205
  77.5 179.0 %all-to-all-done.2 = s32[8,4,32,2048]{3,2,1,0:T(8,128)} async-done(((s32[8,4,32,2048]{3,2,1,0:T(8,128)}), s32[8,4,32,2048]{3,2,1,0:T(8,128)}, u32[]{:S(2)}, u32[]{:S(2)}) %all-to-all-start.2) | async-done | bytes 8388640 | tf_op jit(solution)/shard_map/all_to_all | solution.py:46
  256.5 3.2 all-to-all-start.1
  259.8 7.9 %copy.23 = s32[8,4,32,2048]{3,2,0,1:T(8,128)} copy(s32[8,4,32,2048]{3,2,1,0:T(8,128)} %all-to-all-done.2) | data formatting | bytes 16777216 | tf_op jit(solution)/shard_map/all_to_all | solution.py:46
  267.7 5.7 %all-to-all-start.3 = ((s32[8,4,32,2048]{3,2,0,1:T(8,128)}), s32[8,4,32,2048]{3,2,0,1:T(8,128)}, u32[]{:S(2)}, u32[]{:S(2)}) async-start(s32[8,4,32,2048]{3,2,0,1:T(8,128)} %copy.23), calls=%async_computation.3 | async-start | bytes 16777216 | tf_op jit(solution)/shard_map/all_to_all | solution.py:45
  273.4 0.6 convert_element_type.30
  274.0 0.3 reduce-window.19
  274.7 0.6 dynamic_slice.3
  276.0 0.6 reduce.7
  276.8 6.2 %gather_fusion = f32[1024]{0:T(1024)S(1)} fusion(f32[4096]{0:T(1024)S(1)} %rev.7, s32[1024]{0:T(1024)S(1)} %broadcast_clamp_fusion), kind=kCustom, calls=%fused_computation | custom fusion | bytes 12288 | tf_op jit(solution)/shard_map/gather | solution.py:68
  283.0 4.9 %scatter_custom_fusion.4 = f32[1024]{0:T(1024)} fusion(s32[1024]{0:T(1024)S(1)} %bitcast.51, f32[1024]{0:T(1024)S(1)} %divide_select_fusion, f32[]{:T(128)} %constant.81.clone.1), kind=kCustom, calls=%fused_computation.63 | custom fusion | bytes 4100 | tf_op jit(solution)/shard_map/scatter | solution.py:70
  287.9 78.6 %all-to-all-done.3 = s32[8,4,32,2048]{3,2,0,1:T(8,128)} async-done(((s32[8,4,32,2048]{3,2,0,1:T(8,128)}), s32[8,4,32,2048]{3,2,0,1:T(8,128)}, u32[]{:S(2)}, u32[]{:S(2)}) %all-to-all-start.3) | async-done | bytes 8388640 | tf_op jit(solution)/shard_map/all_to_all | solution.py:45
  366.5 7.7 %copy.24 = s32[8,4,32,2048]{3,2,1,0:T(8,128)} copy(s32[8,4,32,2048]{3,2,0,1:T(8,128)} %all-to-all-done.3) | data formatting | bytes 16777216 | tf_op jit(solution)/shard_map/all_to_all | solution.py:45
  374.2 13.0 %scatter_custom_fusion.3 = s32[1024,2048]{1,0:T(8,128)} fusion(s32[1024]{0:T(1024)S(1)} %bitcast.52, s32[1024,2048]{1,0:T(8,128)} %bitcast.36, s32[]{:T(128)} %constant.83.clone.1), kind=kCustom, calls=%fused_computation.6 | custom fusion | bytes 8389120 | tf_op jit(solution)/shard_map/scatter | solution.py:69
  (29 shorter events, 1.3 us)
Async XLA Ops:
  55.7 13.9 %all-to-all-start = ((s32[8,1,256]{2,1,0:T(1,128)}), s32[8,1,256]{2,1,0:T(1,128)S(1)}, u32[]{:S(2)}, u32[]{:S(2)}) async-start(s32[8,1,256]{2,1,0:T(1,128)} %reshape.203), calls=%async_computation | async-start | bytes 16384 | tf_op jit(solution)/shard_map/all_to_all | solution.py:53
  69.7 186.9 %all-to-all-start.2 = ((s32[8,4,32,2048]{3,2,1,0:T(8,128)}), s32[8,4,32,2048]{3,2,1,0:T(8,128)}, u32[]{:S(2)}, u32[]{:S(2)}) async-start(s32[8,4,32,2048]{3,2,1,0:T(8,128)} %bitcast.35), calls=%async_computation.2 | async-start | bytes 16777216 | tf_op jit(solution)/shard_map/all_to_all | solution.py:46
  256.5 11.1 %all-to-all-start.1 = ((s32[4,1,512]{2,1,0:T(1,128)}), s32[4,1,512]{2,1,0:T(1,128)S(1)}, u32[]{:S(2)}, u32[]{:S(2)}) async-start(s32[4,1,512]{2,1,0:T(1,128)} %reshape.205), calls=%async_computation.1 | async-start | bytes 16384 | tf_op jit(solution)/shard_map/all_to_all | solution.py:52
  267.7 98.8 %all-to-all-start.3 = ((s32[8,4,32,2048]{3,2,0,1:T(8,128)}), s32[8,4,32,2048]{3,2,0,1:T(8,128)}, u32[]{:S(2)}, u32[]{:S(2)}) async-start(s32[8,4,32,2048]{3,2,0,1:T(8,128)} %copy.23), calls=%async_computation.3 | async-start | bytes 16777216 | tf_op jit(solution)/shard_map/all_to_all | solution.py:45
where the time goes:
time: 388 us; the launch traced here: 387 us
  waiting for transfers between devices  258 us (66%)
  local copies, waits for them, and re-layouts  53.9 us (14%)
  blocking collectives  42.1 us (11%)
  starting transfers between devices  20.2 us (5%)
  other arithmetic  11.3 us (3%)
    all_to_all x1, waiting for transfers between devices, body(): lax.all_to_all(send_rows, 'dp', split_axis=0, concat_axis=0, tiled=True)  179 us
    all_to_all x1, waiting for transfers between devices, body(): lax.all_to_all(lax.all_to_all(send_rows, 'dp', split_axis=0, concat_axis=...  78.6 us
    psum x1, blocking collectives, body(): hist = lax.psum(local_hist, ('dp', 'group'))  42.1 us
    scatter x1, local copies, waits for them, and re-layouts, body(): jnp.zeros((capacity, width), jnp.int32).at[target]  13 us
    scatter x1, local copies, waits for them, and re-layouts, body(): jnp.zeros((outside, width), jnp.int32).at[position_send]  8.6 us
    all_to_all x1, local copies, waits for them, and re-layouts, body(): lax.all_to_all(send_rows, 'dp', split_axis=0, concat_axis=0, tiled=True)  7.89 us
  transfers between devices with their start and end apart: 4, of which 2 were waited for; matrix products, arithmetic and copies ran while one was open for 8% of the time, Pallas kernels for 0%

commit v1 on v0

v1 whole, which is shorter than its diff:
```python
import functools

import jax
import jax.numpy as jnp
from jax import lax
from jax.experimental import pallas as pl
from jax.experimental.pallas import tpu as pltpu
from jax.sharding import PartitionSpec as P

BINS = 4096
BIN_WIDTH = 262144
LANES = 128
MESH = pl.DeviceIdType.MESH


def peer(me, i, n):
    return lax.rem(me + 1 + lax.rem(i + n // 2 - 1, n - 1), n)


def place(d, n_member):
    return (lax.div(d, n_member), lax.rem(d, n_member))


def greet(me, n, n_member):
    barrier = pltpu.get_barrier_semaphore()

    def signal(i, c):
        pl.semaphore_signal(
            barrier, inc=1, device_id=place(peer(me, i, n), n_member), device_id_type=MESH
        )
        return c

    lax.fori_loop(0, n - 1, signal, 0)
    pl.semaphore_wait(barrier, n - 1)


def meta_kernel(n, n_member, mine, every, local_sem, send_sem, recv_sem):
    me = lax.axis_index("dp") * n_member + lax.axis_index("group")
    own = pltpu.make_async_copy(mine, every.at[me], local_sem)
    own.start()
    greet(me, n, n_member)

    def copy_to(d, sem):
        return pltpu.make_async_remote_copy(
            src_ref=mine,
            dst_ref=every.at[me],
            send_sem=send_sem.at[d],
            recv_sem=recv_sem.at[me],
            device_id=place(d, n_member),
            device_id_type=MESH,
        )

    def start(i, c):
        d = peer(me, i, n)
        copy_to(d, d).start()
        return c

    def finish(i, c):
        d = peer(me, i, n)
        copy = pltpu.make_async_remote_copy(
            src_ref=mine,
            dst_ref=every.at[d],
            send_sem=send_sem.at[d],
            recv_sem=recv_sem.at[d],
            device_id=place(d, n_member),
            device_id_type=MESH,
        )
        copy.wait_send()
        copy.wait_recv()
        return c

    lax.fori_loop(0, n - 1, start, 0)
    own.wait()
    lax.fori_loop(0, n - 1, finish, 0)


def rows_kernel(
    n, n_member, slots, pieces,
    index, tokens, key_send, keys_all,
    got, got_keys, hist,
    held, send, load_sem, own_sem, send_sem, recv_sem, ksend_sem, krecv_sem,
):
    me = lax.axis_index("dp") * n_member + lax.axis_index("group")
    loads = [
        pltpu.make_async_copy(
            tokens.at[:, pl.ds(p * LANES, LANES)], held.at[:, p, :], load_sem.at[p]
        )
        for p in range(pieces)
    ]
    for load in loads:
        load.start()
    greet(me, n, n_member)
    for load in loads:
        load.wait()

    def block(d):
        return pl.ds(d * slots, slots)

    def gather(d):
        for j in range(slots):
            send[d * slots + j] = held[index[d * slots + j]]

    def copies(d, at):
        rows = pltpu.make_async_remote_copy(
            src_ref=send.at[block(d)],
            dst_ref=got.at[block(at)],
            send_sem=send_sem.at[d],
            recv_sem=recv_sem.at[at],
            device_id=place(d, n_member),
            device_id_type=MESH,
        )
        keys = pltpu.make_async_remote_copy(
            src_ref=key_send.at[d],
            dst_ref=got_keys.at[at],
            send_sem=ksend_sem.at[d],
            recv_sem=krecv_sem.at[at],
            device_id=place(d, n_member),
            device_id_type=MESH,
        )
        return rows, keys

    gather(peer(me, 0, n))

    def start(i, c):
        gather(peer(me, i + 1, n))
        for copy in copies(peer(me, i, n), me):
            copy.start()
        return c

    lax.fori_loop(0, n - 2, start, 0)
    gather(me)
    for copy in copies(peer(me, n - 2, n), me):
        copy.start()
    own = pltpu.make_async_copy(send.at[block(me)], got.at[block(me)], own_sem.at[0])
    own_keys = pltpu.make_async_copy(key_send.at[me], got_keys.at[me], own_sem.at[1])
    own.start()
    own_keys.start()

    hist[...] = jnp.zeros_like(hist)
    hi_of = lax.broadcasted_iota(jnp.int32, (BINS // LANES, LANES), 0)
    lo_of = lax.broadcasted_iota(jnp.int32, (LANES, LANES), 0)

    def count(r, c):
        bins = keys_all[pl.ds(r, 1), :] // BIN_WIDTH
        hi = jnp.where(hi_of == bins // LANES, 1.0, 0.0).astype(jnp.bfloat16)
        lo = jnp.where(lo_of == bins % LANES, 1.0, 0.0).astype(jnp.bfloat16)
        hist[...] += lax.dot_general(
            hi, lo, (((1,), (1,)), ((), ())), preferred_element_type=jnp.float32
        )
        return c

    lax.fori_loop(0, keys_all.shape[0], count, 0)

    own.wait()
    own_keys.wait()

    def finish(i, c):
        d = peer(me, i, n)
        for copy in copies(d, d):
            copy.wait_send()
            copy.wait_recv()
        return c

    lax.fori_loop(0, n - 1, finish, 0)


def pack_kernel(pieces, chunk, index, got, out, held, made, load_sem, out_sem):
    rows = got.shape[0]
    load = pltpu.make_async_copy(got, held.at[pl.ds(0, rows)], load_sem)
    load.start()
    held[rows] = jnp.zeros(held.shape[1:], jnp.int32)
    load.wait()

    def stores(k):
        return [
            pltpu.make_async_copy(
                made.at[pl.ds(k * chunk, chunk), p, :],
                out.at[pl.ds(k * chunk, chunk), pl.ds(p * LANES, LANES)],
                out_sem.at[k, p],
            )
            for p in range(pieces)
        ]

    def fill(k):
        def some(g, c):
            for j in range(8):
                s = k * chunk + g * 8 + j
                made[s] = held[index[s]]
            return c

        lax.fori_loop(0, chunk // 8, some, 0)

    def step(k, c):
        fill(k)
        for copy in stores(k):
            copy.start()
        return c

    def finish(k, c):
        for copy in stores(k):
            copy.wait()
        return c

    lax.fori_loop(0, rows // chunk, step, 0)
    lax.fori_loop(0, rows // chunk, finish, 0)


def body(n_owner, n_member, keys, cut, owner, tokens):
    examples, width = tokens.shape
    n = n_owner * n_member
    slots = 2 * examples // n
    capacity = 2 * examples
    pieces = width // LANES
    per = examples // LANES
    me_dp, me_group = lax.axis_index("dp"), lax.axis_index("group")
    me = me_dp * n_member + me_group
    vmem = pl.BlockSpec(memory_space=pltpu.VMEM)
    smem = pl.BlockSpec(memory_space=pltpu.SMEM)
    hbm = pl.BlockSpec(memory_space=pl.ANY)
    dest = owner[:, 0]

    mine = jnp.concatenate([keys.reshape(per, LANES), dest.reshape(per, LANES)], axis=0)
    every = pl.pallas_call(
        functools.partial(meta_kernel, n, n_member),
        out_shape=jax.ShapeDtypeStruct((n, 2 * per, LANES), jnp.int32),
        in_specs=[vmem],
        out_specs=vmem,
        scratch_shapes=[
            pltpu.SemaphoreType.DMA,
            pltpu.SemaphoreType.DMA((n,)),
            pltpu.SemaphoreType.DMA((n,)),
        ],
        compiler_params=pltpu.CompilerParams(collective_id=0, has_side_effects=True),
    )(mine)
    keys_all = every[:, :per].reshape(n * per, LANES)
    owner_all = every[:, per:].reshape(n, examples)
    kept_all = keys_all.reshape(n, examples) // BIN_WIDTH >= cut[0]
    code_all = jnp.where(kept_all, owner_all, -1)
    table = jnp.sum(
        code_all[:, None, :] == jnp.arange(n_owner, dtype=jnp.int32)[None, :, None],
        axis=2, dtype=jnp.int32,
    )
    source = jnp.arange(n, dtype=jnp.int32)
    before = jnp.sum(jnp.where((source < me)[:, None], table, 0), axis=0)

    code = jnp.where(keys // BIN_WIDTH >= cut[0], dest, -1)
    e = jnp.arange(examples, dtype=jnp.int32)
    local_rank = jnp.sum(
        (code[:, None] == code[None, :]) & (e[None, :] < e[:, None]), axis=1, dtype=jnp.int32
    )
    spot = jnp.where(code >= 0, code * capacity + local_rank, -1)
    want = (
        jnp.arange(n_owner, dtype=jnp.int32)[:, None, None] * capacity
        + ((jnp.arange(n_member, dtype=jnp.int32)[None, :] - before[:, None]) % n_member)[:, :, None]
        + jnp.arange(slots, dtype=jnp.int32)[None, None, :] * n_member
    ).reshape(-1)
    match = want[:, None] == spot[None, :]
    index = jnp.sum(jnp.where(match, e[None, :], 0), axis=1)
    key_send = jnp.sum(jnp.where(match, keys[None, :], 0), axis=1)
    key_send = jnp.pad(key_send.reshape(n, 1, slots), ((0, 0), (0, 0), (0, LANES - slots)))

    got, got_keys, hist = pl.pallas_call(
        functools.partial(rows_kernel, n, n_member, slots, pieces),
        out_shape=(
            jax.ShapeDtypeStruct((capacity, pieces, LANES), jnp.int32),
            jax.ShapeDtypeStruct((n, 1, LANES), jnp.int32),
            jax.ShapeDtypeStruct((BINS // LANES, LANES), jnp.float32),
        ),
        in_specs=[smem, hbm, vmem, vmem],
        out_specs=(hbm, vmem, vmem),
        scratch_shapes=[
            pltpu.VMEM((examples, pieces, LANES), jnp.int32),
            pltpu.VMEM((capacity, pieces, LANES), jnp.int32),
            pltpu.SemaphoreType.DMA((pieces,)),
            pltpu.SemaphoreType.DMA((2,)),
            pltpu.SemaphoreType.DMA((n,)),
            pltpu.SemaphoreType.DMA((n,)),
            pltpu.SemaphoreType.DMA((n,)),
            pltpu.SemaphoreType.DMA((n,)),
        ],
        compiler_params=pltpu.CompilerParams(
            collective_id=1, has_side_effects=True, vmem_limit_bytes=60 * 1024 * 1024
        ),
    )(index, tokens, key_send, keys_all)
    hist = hist.reshape(BINS)

    arrived = jnp.sum(
        jnp.where(jnp.arange(n_owner, dtype=jnp.int32)[None, :] == me_dp, table, 0), axis=1
    )
    through = jnp.sum(jnp.where(source[None, :] <= source[:, None], arrived[None, :], 0), axis=1)
    rank = jnp.arange(capacity, dtype=jnp.int32) * n_member + me_group
    past = through[None, :] <= rank[:, None]
    origin = jnp.sum(past, axis=1, dtype=jnp.int32)
    start = jnp.sum(jnp.where(past, arrived[None, :], 0), axis=1)
    valid = origin < n
    pick = jnp.where(valid, origin * slots + (rank - start) // n_member, capacity)

    packed_rows = pl.pallas_call(
        functools.partial(pack_kernel, pieces, LANES),
        out_shape=jax.ShapeDtypeStruct((capacity, width), jnp.int32),
        in_specs=[smem, hbm],
        out_specs=hbm,
        scratch_shapes=[
            pltpu.VMEM((capacity + 1, pieces, LANES), jnp.int32),
            pltpu.VMEM((capacity, pieces, LANES), jnp.int32),
            pltpu.SemaphoreType.DMA,
            pltpu.SemaphoreType.DMA((capacity // LANES, pieces)),
        ],
        compiler_params=pltpu.CompilerParams(vmem_limit_bytes=60 * 1024 * 1024),
    )(pick, got)

    b = jnp.arange(BINS, dtype=jnp.int32)
    total = jnp.maximum(jnp.sum(jnp.where(b >= cut[0], hist, 0.0)), 1.0)
    bins = got_keys[:, 0, :slots].reshape(-1) // BIN_WIDTH
    above = jnp.sum(jnp.where(b[None, :] >= bins[:, None], hist[None, :], 0.0), axis=1)
    place_of = jnp.arange(capacity, dtype=jnp.int32)
    value = jnp.sum(jnp.where(pick[:, None] == place_of[None, :], above[None, :], 0.0), axis=1)
    packed_weights = value / total
    return (hist.astype(jnp.int32), packed_rows, packed_weights)


def solution(mesh):
    placed = (P(("dp", "group")), P(), P(("dp", "group"), None), P(("dp", "group"), None))
    return jax.shard_map(
        functools.partial(body, mesh.shape["dp"], mesh.shape["group"]),
        mesh=mesh,
        in_specs=placed,
        out_specs=(P(), P(("dp", "group"), None), P(("dp", "group"))),
        check_vma=False,
    )
```

time: 388 us -> 233 us (0.60)
  waiting for transfers between devices: 258 us -> 0 us
  Pallas kernels: 0 us -> 216 us
  local copies, waits for them, and re-layouts: 53.9 us -> 2.64 us
  blocking collectives: 42.1 us -> 0 us
  starting transfers between devices: 20.2 us -> 0 us
    all_to_all x4 -> x0, waiting for transfers between devices: 258 us -> none  [the longest x1 179 us: body(): lax.all_to_all(send_rows, 'dp', split_axis=0, concat_axis=0, tiled=True)]
    pallas_call x0 -> x3, Pallas kernels: none -> 216 us  [the longest x1 194 us: body(): pl.pallas_call(functools.partial(rows_kernel, n, n_member, slots, pieces)...]
    psum x1 -> x0, blocking collectives: 42.1 us -> none  [body(): hist = lax.psum(local_hist, ('dp', 'group'))]
    scatter x4 -> x0, local copies, waits for them, and re-layouts: 28.4 us -> none  [the longest x1 13 us: body(): jnp.zeros((capacity, width), jnp.int32).at[target]]
    all_to_all x4 -> x0, starting transfers between devices: 20.2 us -> none  [the longest x1 6 us: body(): lax.all_to_all(send_rows, 'dp', split_axis=0, concat_axis=0, tiled=True)]
    all_to_all x5 -> x0, local copies, waits for them, and re-layouts: 16.1 us -> none  [the longest x1 7.89 us: body(): lax.all_to_all(send_rows, 'dp', split_axis=0, concat_axis=0, tiled=True)]
    reduce_sum x3 -> x9, other arithmetic: 1.68 us -> 8.78 us  [the longest x1 3 us: body(): jnp.sum(jnp.where(b[None, :] >= bins[:, None], hist[None, :], 0.0), axis=1)]
    gather x1 -> x0, local copies, waits for them, and re-layouts: 6.15 us -> none  [body(): weight = jnp.where(valid, suffix[got_bins] / total, 0.0)]
  transfers between devices with their start and end apart: 4 -> 0, of which waited for: 2 -> 0; matrix products, arithmetic and copies ran while one was open for 8% -> 0% of each run, Pallas kernels for 0% -> 0%
where the time goes in v1:
time: 233 us
  Pallas kernels  216 us (93%)
  other arithmetic  11.7 us (5%)
  local copies, waits for them, and re-layouts  2.64 us (1%)
    pallas_call x1, Pallas kernels, body(): pl.pallas_call(functools.partial(rows_kernel, n, n_member, slots, pieces)...  194 us
    pallas_call x1, Pallas kernels, body(): pl.pallas_call(functools.partial(meta_kernel, n, n_member), out_shape=jax...  13.6 us
    pallas_call x1, Pallas kernels, body(): pl.pallas_call(functools.partial(pack_kernel, pieces, LANES), out_shape=j...  8.67 us

profile of v1, /device:TPU:0, one launch (start us, length us, event | category | flops | bytes accessed | tf_op | source)
XLA Modules:
  0.0 232.6 jit_solution(6470960027333049995)
XLA Ops:
  0.6 1.3 pad_add_fusion.mine
  1.9 13.6 %shard_map.67 = s32[32,8,128]{2,1,0:T(8,128)} custom-call(s32[8,128]{1,0:T(8,128)} %pad_add_fusion.mine), custom_call_target="tpu_custom_call" | custom-call | tf_op jit(solution)/shard_map/pallas_call | solution.py:223
  15.5 1.0 fusion.24
  16.5 0.0 copy-start
  17.3 0.6 convert_reduce_fusion.1
  17.9 0.1 select_reduce_fusion.4
  18.1 0.1 fusion.10
  18.1 0.1 broadcast_add_fusion
  18.2 0.1 add.95
  18.3 0.7 fusion.23
  19.0 0.3 convert_reduce_fusion
  19.3 2.0 fusion.1
  21.3 0.1 reshape.208
  21.4 0.6 pad.4.key_send
  22.0 0.0 copy-done
  22.0 194.0 %shard_map.68 = (s32[1024,16,128]{2,1,0:T(8,128)}, s32[32,1,128]{2,1,0:T(1,128)}, f32[32,128]{1,0:T(8,128)}) custom-call(s32[1024]{0:T(1024)} %get-tuple-element.12.index, s32[512,2048]{1,0:T(8,128)} %tokens.1, s32[32,1,128]{2,1,0:T(1,128)} %pad.4.key_send, s32[128,128]{1,0:T(8,128)} %bitcast.33), custom_call_target="tpu_custom_call" | custom-call | tf_op jit(solution)/shard_map/pallas_call | solution.py:262
  216.0 0.8 slice_reduce_fusion
  216.7 0.1 reshape_squeeze.7
  216.8 3.0 %select_reduce_fusion = f32[1024]{0:T(1024)S(1)} fusion(f32[4096]{0:T(1024)} %bitcast.36, s32[1024]{0:T(1024)S(1)} %add_select_fusion.1), kind=kLoop, calls=%fused_computation | loop fusion | flops 12581888 | bytes 24576 | tf_op jit(solution)/shard_map/reduce_sum | solution.py:315
  219.8 0.1 select_reduce_fusion.3
  220.0 0.1 fusion.4
  220.1 0.0 copy-start.1
  220.1 0.7 select_reduce_fusion.1
  220.8 1.9 select_reduce_fusion.2
  223.3 0.6 broadcast_divide_fusion
  223.9 0.0 copy-done.1
  223.9 8.7 %shard_map.69 = s32[1024,2048]{1,0:T(8,128)} custom-call(s32[1024]{0:T(1024)} %copy-done.1, s32[1024,16,128]{2,1,0:T(8,128)} %get-tuple-element.7.got), custom_call_target="tpu_custom_call" | custom-call | tf_op jit(solution)/shard_map/pallas_call | solution.py:298
  (9 shorter events, 0.1 us)
Async XLA Ops:
  16.5 5.4 %copy-start = (s32[32,4,128]{2,1,0:T(4,128)}, s32[32,4,128]{2,1,0:T(4,128)S(1)}, u32[]{:S(2)}) copy-start(s32[32,4,128]{2,1,0:T(4,128)S(1)} %get-tuple-element.15) | copy-start | bytes 196612
  220.1 3.8 %copy-start.1 = (s32[1024]{0:T(1024)}, s32[1024]{0:T(1024)S(1)}, u32[]{:S(2)}) copy-start(s32[1024]{0:T(1024)S(1)} %fusion.13.index) | copy-start | bytes 12292
